TPU v7x, 64 devices: a 2x2x8 block of a 4x4x8 slice. The times are simulated.
64 devices in a mesh: dp: 8 (over x, y, core), tp: 8 (over z).
Axes of the slice: x: 2, y: 2, z: 8, core: 2. Of those that a mesh axis runs over, the one named last changes fastest.
The devices are a block of a 4x4x8 slice.
Arguments:
- x: bfloat16 [16384, 4096], P('dp'), parts along dimension 0
- w_gate: bfloat16 [4096, 14336], P(None, 'tp')
- w_up: bfloat16 [4096, 14336], P(None, 'tp')
- w_down: bfloat16 [14336, 4096], P('tp')
Outputs:
- output: bfloat16 [16384, 4096], P('dp'), parts along dimension 0
There are 8 independent parts. A program takes and returns all parts, laid end to end along the dimension named above; an argument that names none is the same for every part.
All inputs are finite; a program needn't handle non-finite values.
Results may differ from a plain program's by a relative error of at most 0.016.
Values are sent between devices in bfloat16 or wider.
A program may use at most 768 MiB of HBM per device.

v0:
```python
import jax
import jax.numpy as jnp
from jax import lax
from jax.sharding import PartitionSpec as P


def solution(mesh):
    def step(x, w_gate, w_up, w_down):
        gate = jnp.dot(x, w_gate, preferred_element_type=jnp.float32)
        up = jnp.dot(x, w_up, preferred_element_type=jnp.float32)
        hidden = (jax.nn.silu(gate) * up).astype(jnp.bfloat16)
        term = jnp.dot(hidden, w_down, preferred_element_type=jnp.float32).astype(jnp.bfloat16)
        return lax.psum(term, "tp")

    return jax.shard_map(
        step,
        mesh=mesh,
        in_specs=(P("dp", None), P(None, "tp"), P(None, "tp"), P("tp", None)),
        out_specs=P("dp", None),
        check_vma=False,
    )
```

profile of v0, /device:TPU:21, one launch (start us, length us, event | category | flops | bytes accessed | tf_op | source)
XLA Modules:
  0.0 484.1 jit_solution(4251871822191283609)
XLA Ops:
  6.5 0.0 all-reduce.2.cloned.1.call-start
  6.6 39.2 %fusion = f32[2048,1792]{1,0:T(8,128)} fusion(bf16[2048,4096]{1,0:T(8,128)(2,1)} %param.4, bf16[4096,1792]{1,0:T(8,128)(2,1)} %param.5), kind=kOutput, calls=%fused_computation.2 | convolution fusion | flops 30064771072 | bytes 46137344 | tf_op jit(solution)/shard_map/dot_general | solution.py:9
  45.8 38.9 %multiply_convert_fusion = bf16[2048,1792]{1,0:T(8,128)(2,1)S(1)} fusion(f32[2048,1792]{1,0:T(8,128)} %fusion, bf16[2048,4096]{1,0:T(8,128)(2,1)} %param.4, bf16[4096,1792]{1,0:T(8,128)(2,1)} %param.6), kind=kOutput, calls=%fused_computation.1 | convolution fusion | flops 30086791168 | bytes 53477376 | tf_op jit(solution)/shard_map/dot_general | solution.py:10
  84.7 35.5 %convolution_convert_fusion = bf16[2048,4096]{1,0:T(8,128)(2,1)} fusion(bf16[2048,1792]{1,0:T(8,128)(2,1)S(1)} %multiply_convert_fusion, bf16[1792,4096]{1,0:T(8,128)(2,1)} %param.7), kind=kOutput, calls=%fused_computation | convolution fusion | flops 30073159680 | bytes 38797312 | tf_op jit(solution)/shard_map/dot_general | solution.py:12
  120.2 0.1 all-reduce.2.cloned.1.call-update
  120.2 343.0 %all-reduce.2.cloned.1.call-done = bf16[2048,4096]{1,0:T(8,128)(2,1)} async-done(((bf16[2048,4096]{1,0:T(8,128)(2,1)}), bf16[2048,4096]{1,0:T(8,128)(2,1)}) %all-reduce.2.cloned.1.call-update) | async-done | bytes 16777232 | tf_op jit(solution)/shard_map/psum | solution.py:13
  463.2 14.1 %copy.6 = bf16[2048,4096]{1,0:T(8,128)(2,1)} copy(bf16[2048,4096]{1,0:T(8,128)(2,1)} %all-reduce.2.cloned.1.call-done) | data formatting | bytes 33554432
Async XLA Ops:
  6.5 456.7 %all-reduce.2.cloned.1.call-start = ((), (), s32[]{:S(2)}) async-start(), calls=%async_computation | async-start | bytes 33554432 | tf_op jit(solution)/shard_map/psum | solution.py:13
Sparse Core Ops, SparseCore 0:
  120.4 342.8 all-reduce.1
where the time goes:
time: 484 us
  waiting for transfers between devices  343 us (71%)
  matrix products  114 us (24%)
  local copies, waits for them, and re-layouts  14.1 us (3%)
  between operations  13.4 us (3%)
    psum x1, waiting for transfers between devices, step(): return lax.psum(term, 'tp')  343 us
    dot_general x1, matrix products, step(): gate = jnp.dot(x, w_gate, preferred_element_type=jnp.float32)  39.2 us
    dot_general x1, matrix products, step(): up = jnp.dot(x, w_up, preferred_element_type=jnp.float32)  38.9 us
    dot_general x1, matrix products, step(): jnp.dot(hidden, w_down, preferred_element_type=jnp.float32)  35.5 us
    unnamed x1, local copies, waits for them, and re-layouts  14.1 us
  transfers between devices with their start and end apart: 1, of which 1 were waited for; matrix products, arithmetic and copies ran while one was open for 0% of the time, Pallas kernels for 0%

commit v1 on v0

v1 whole, which is shorter than its diff:
```python
import functools

import jax
import jax.numpy as jnp
from jax import lax
from jax.experimental import pallas as pl
from jax.experimental.pallas import tpu as pltpu
from jax.sharding import PartitionSpec as P

MESH = pl.DeviceIdType.MESH
AXIS = "tp"


def kernel(
    n, x_hbm, wg_hbm, wu_hbm, wd_hbm, y, xv, wg, wu, wd, hidden, x_sem, up_sem, down_sem, send_sem, recv_sem
):
    me = lax.axis_index(AXIS)
    right, left = lax.rem(me + 1, n), lax.rem(me + n - 1, n)
    half = xv.shape[0] // 2
    up_tiles, _, up_tile = wg.shape
    down_tiles, _, down_tile = wd.shape

    def shard(direction, step):
        if direction == 0:
            return lax.rem(me + 2 * n - 1 - step, n)
        return lax.rem(me + 1 + step, n)

    def rows(direction, j):
        return pl.ds(pl.multiple_of(j * 2 * half + direction * half, half), half)

    def x_copy(direction, step):
        return pltpu.make_async_copy(
            x_hbm.at[rows(direction, shard(direction, step)), :],
            xv.at[pl.ds(direction * half, half), :],
            x_sem.at[direction],
        )

    def up_copies(t):
        columns = pl.ds(pl.multiple_of(t * up_tile, up_tile), up_tile)
        return [
            pltpu.make_async_copy(hbm.at[:, columns], vmem.at[t], up_sem.at[k, t])
            for k, (hbm, vmem) in enumerate(((wg_hbm, wg), (wu_hbm, wu)))
        ]

    def down_copy(t):
        columns = pl.ds(pl.multiple_of(t * down_tile, down_tile), down_tile)
        return pltpu.make_async_copy(wd_hbm.at[:, columns], wd.at[t], down_sem.at[t])

    def hop(direction, j, t):
        block = y.at[rows(direction, j), pl.ds(pl.multiple_of(t * down_tile, down_tile), down_tile)]
        return pltpu.make_async_remote_copy(
            src_ref=block,
            dst_ref=block,
            send_sem=send_sem.at[direction, j, t],
            recv_sem=recv_sem.at[direction, j, t],
            device_id={AXIS: right if direction == 0 else left},
            device_id_type=MESH,
        )

    def project_up(first):
        def tile(t, _):
            if first:
                for copy in up_copies(t):
                    copy.wait()
            gate = jnp.dot(xv[...], wg[t], preferred_element_type=jnp.float32)
            up = jnp.dot(xv[...], wu[t], preferred_element_type=jnp.float32)
            columns = pl.ds(pl.multiple_of(t * up_tile, up_tile), up_tile)
            hidden[:, columns] = (jax.nn.silu(gate) * up).astype(hidden.dtype)
            return 0

        lax.fori_loop(0, up_tiles, tile, 0)

    def project_down(first, step):
        js = [shard(d, step) for d in (0, 1)]
        before = [shard(d, step - 1) for d in (0, 1)]

        def tile(t, _):
            if first:
                down_copy(t).wait()
            term = jnp.dot(hidden[...], wd[t], preferred_element_type=jnp.float32)
            columns = pl.ds(pl.multiple_of(t * down_tile, down_tile), down_tile)
            for d in (0, 1):
                total = term[d * half : (d + 1) * half, :]
                if not first:
                    hop(d, js[d], t).wait_recv()
                    hop(d, before[d], t).wait_send()
                    total = total + y[rows(d, js[d]), columns].astype(jnp.float32)
                y[rows(d, js[d]), columns] = total.astype(y.dtype)

            @pl.when(t > 0)
            def _():
                for d in (0, 1):
                    hop(d, js[d], t - 1).start()

            return 0

        lax.fori_loop(0, down_tiles, tile, 0)
        for d in (0, 1):
            hop(d, js[d], down_tiles - 1).start()

    barrier = pltpu.get_barrier_semaphore()
    for neighbour in (left, right):
        pl.semaphore_signal(barrier, inc=1, device_id={AXIS: neighbour}, device_id_type=MESH)

    for d in (0, 1):
        x_copy(d, 0).start()

    def start_up(t, _):
        for copy in up_copies(t):
            copy.start()
        return 0

    lax.fori_loop(0, up_tiles, start_up, 0)

    def start_down(t, _):
        down_copy(t).start()
        return 0

    lax.fori_loop(0, down_tiles, start_down, 0)

    for d in (0, 1):
        x_copy(d, 0).wait()
    project_up(True)
    for d in (0, 1):
        x_copy(d, 1).start()
    pl.semaphore_wait(barrier, 2)
    project_down(True, 0)

    def reduce_step(step, _):
        for d in (0, 1):
            x_copy(d, step).wait()
        project_up(False)

        @pl.when(step < n - 1)
        def _():
            for d in (0, 1):
                x_copy(d, step + 1).start()

        project_down(False, step)
        return 0

    lax.fori_loop(1, n, reduce_step, 0)

    def gather_step(step, _):
        js = [lax.rem(me + n - step, n), lax.rem(me + step, n)]
        before = [lax.rem(me + n - step + 1, n), lax.rem(me + step - 1, n)]

        def tile(t, _):
            for d in (0, 1):
                hop(d, js[d], t).wait_recv()

                @pl.when(step < n - 1)
                def _():
                    hop(d, js[d], t).start()

                hop(d, before[d], t).wait_send()
            return 0

        return lax.fori_loop(0, down_tiles, tile, 0)

    lax.fori_loop(1, n, gather_step, 0)


def solution(mesh):
    n = mesh.shape[AXIS]

    def step(x, w_gate, w_up, w_down):
        tokens, d_model = x.shape
        hidden = w_gate.shape[1]
        block = tokens // n
        up_tile, down_tile = 256, 512
        up_tiles, down_tiles = hidden // up_tile, d_model // down_tile
        y = pl.pallas_call(
            functools.partial(kernel, n),
            out_shape=pltpu.VMEM((tokens, d_model), jnp.bfloat16),
            in_specs=[pl.BlockSpec(memory_space=pl.ANY)] * 4,
            out_specs=pl.BlockSpec(memory_space=pltpu.VMEM),
            scratch_shapes=[
                pltpu.VMEM((block, d_model), jnp.bfloat16),
                pltpu.VMEM((up_tiles, d_model, up_tile), jnp.bfloat16),
                pltpu.VMEM((up_tiles, d_model, up_tile), jnp.bfloat16),
                pltpu.VMEM((down_tiles, hidden, down_tile), jnp.bfloat16),
                pltpu.VMEM((block, hidden), jnp.bfloat16),
                pltpu.SemaphoreType.DMA((2,)),
                pltpu.SemaphoreType.DMA((2, up_tiles)),
                pltpu.SemaphoreType.DMA((down_tiles,)),
                pltpu.SemaphoreType.DMA((2, n, down_tiles)),
                pltpu.SemaphoreType.DMA((2, n, down_tiles)),
            ],
            compiler_params=pltpu.CompilerParams(
                collective_id=0, has_side_effects=True, vmem_limit_bytes=47 << 20
            ),
            name="mlp_ring",
        )(x, w_gate, w_up, w_down)
        return y

    return jax.shard_map(
        step,
        mesh=mesh,
        in_specs=(P("dp", None), P(None, AXIS), P(None, AXIS), P(AXIS, None)),
        out_specs=P("dp", None),
        check_vma=False,
    )
```

time: 484 us -> 345 us (0.71)
  waiting for transfers between devices: 343 us -> 0 us
  Pallas kernels: 0 us -> 338 us
  matrix products: 114 us -> 0 us
  between operations: 13.4 us -> 0.01 us
  local copies, waits for them, and re-layouts: 14.1 us -> 6.16 us
    psum x1 -> x0, waiting for transfers between devices: 343 us -> none  [step(): return lax.psum(term, 'tp')]
    pallas_call x0 -> x1, Pallas kernels: none -> 338 us  [step(): pl.pallas_call(functools.partial(kernel, n), out_shape=pltpu.VMEM((tokens...]
    dot_general x3 -> x0, matrix products: 114 us -> none  [the longest x1 39.2 us: step(): gate = jnp.dot(x, w_gate, preferred_element_type=jnp.float32)]
    unnamed x1, local copies, waits for them, and re-layouts: 14.1 us -> 6.16 us
  transfers between devices with their start and end apart: 1 -> 0, of which waited for: 1 -> 0; matrix products, arithmetic and copies ran while one was open for 0% -> 0% of each run, Pallas kernels for 0% -> 0%
where the time goes in v1:
time: 345 us
  Pallas kernels  338 us (98%)
  local copies, waits for them, and re-layouts  6.16 us (2%)
    pallas_call x1, Pallas kernels, step(): pl.pallas_call(functools.partial(kernel, n), out_shape=pltpu.VMEM((tokens...  338 us

profile of v1, /device:TPU:21, one launch (start us, length us, event | category | flops | bytes accessed | tf_op | source)
XLA Modules:
  0.0 344.5 jit_solution(7815034452218790506)
XLA Ops:
  0.0 338.4 %mlp_ring.1 = bf16[2048,4096]{1,0:T(8,128)(2,1)S(1)} custom-call(bf16[2048,4096]{1,0:T(8,128)(2,1)} %x_hbm.1, bf16[4096,1792]{1,0:T(8,128)(2,1)} %wg_hbm.1, bf16[4096,1792]{1,0:T(8,128)(2,1)} %wu_hbm.1, bf16[1792,4096]{1,0:T(8,128)(2,1)} %wd_hbm.1), custom_call_target="tpu_custom_call" | custom-call | tf_op jit(solution)/shard_map/mlp_ring/pallas_call | solution.py:173
  338.4 6.2 %copy.6 = bf16[2048,4096]{1,0:T(8,128)(2,1)} copy(bf16[2048,4096]{1,0:T(8,128)(2,1)S(1)} %mlp_ring.1) | data formatting | bytes 33554432

commit v2 on v1

--- a/solution.py
+++ b/solution.py
@@ -9,6 +9,21 @@
 
 MESH = pl.DeviceIdType.MESH
 AXIS = "tp"
+
+
+def gathered(n):
+    return n - 1 - lax.rem(lax.axis_index("dp"), 2)
+
+
+def half_rows(half, direction, j):
+    return pl.ds(pl.multiple_of(j * 2 * half + direction * half, half), half)
+
+
+def greet(me, n):
+    barrier = pltpu.get_barrier_semaphore()
+    for neighbour in (lax.rem(me + 1, n), lax.rem(me + n - 1, n)):
+        pl.semaphore_signal(barrier, inc=1, device_id={AXIS: neighbour}, device_id_type=MESH)
+    return barrier
 
 
 def kernel(
@@ -26,7 +41,7 @@
         return lax.rem(me + 1 + step, n)
 
     def rows(direction, j):
-        return pl.ds(pl.multiple_of(j * 2 * half + direction * half, half), half)
+        return half_rows(half, direction, j)
 
     def x_copy(direction, step):
         return pltpu.make_async_copy(
@@ -46,13 +61,13 @@
         columns = pl.ds(pl.multiple_of(t * down_tile, down_tile), down_tile)
         return pltpu.make_async_copy(wd_hbm.at[:, columns], wd.at[t], down_sem.at[t])
 
-    def hop(direction, j, t):
+    def hop(direction, j, t, count):
         block = y.at[rows(direction, j), pl.ds(pl.multiple_of(t * down_tile, down_tile), down_tile)]
         return pltpu.make_async_remote_copy(
             src_ref=block,
             dst_ref=block,
-            send_sem=send_sem.at[direction, j, t],
-            recv_sem=recv_sem.at[direction, j, t],
+            send_sem=send_sem.at[direction, t],
+            recv_sem=recv_sem.at[direction, lax.rem(count, 2), t],
             device_id={AXIS: right if direction == 0 else left},
             device_id_type=MESH,
         )
@@ -79,28 +94,28 @@
                 down_copy(t).wait()
             term = jnp.dot(hidden[...], wd[t], preferred_element_type=jnp.float32)
             columns = pl.ds(pl.multiple_of(t * down_tile, down_tile), down_tile)
+            if not first:
+                for d in (0, 1):
+                    hop(d, js[d], t, step - 1).wait_recv()
+                    hop(d, before[d], t, step - 1).wait_send()
             for d in (0, 1):
                 total = term[d * half : (d + 1) * half, :]
                 if not first:
-                    hop(d, js[d], t).wait_recv()
-                    hop(d, before[d], t).wait_send()
                     total = total + y[rows(d, js[d]), columns].astype(jnp.float32)
                 y[rows(d, js[d]), columns] = total.astype(y.dtype)
 
             @pl.when(t > 0)
             def _():
                 for d in (0, 1):
-                    hop(d, js[d], t - 1).start()
+                    hop(d, js[d], t - 1, step).start()
 
             return 0
 
         lax.fori_loop(0, down_tiles, tile, 0)
         for d in (0, 1):
-            hop(d, js[d], down_tiles - 1).start()
-
-    barrier = pltpu.get_barrier_semaphore()
-    for neighbour in (left, right):
-        pl.semaphore_signal(barrier, inc=1, device_id={AXIS: neighbour}, device_id_type=MESH)
+            hop(d, js[d], down_tiles - 1, step).start()
+
+    barrier = greet(me, n)
 
     for d in (0, 1):
         x_copy(d, 0).start()
@@ -141,24 +156,88 @@
 
     lax.fori_loop(1, n, reduce_step, 0)
 
+    last = gathered(n)
+
     def gather_step(step, _):
         js = [lax.rem(me + n - step, n), lax.rem(me + step, n)]
         before = [lax.rem(me + n - step + 1, n), lax.rem(me + step - 1, n)]
 
         def tile(t, _):
             for d in (0, 1):
-                hop(d, js[d], t).wait_recv()
-
-                @pl.when(step < n - 1)
-                def _():
-                    hop(d, js[d], t).start()
-
-                hop(d, before[d], t).wait_send()
+                hop(d, js[d], t, n - 2 + step).wait_recv()
+                hop(d, before[d], t, n - 2 + step).wait_send()
+
+            @pl.when(step < last)
+            def _():
+                for d in (0, 1):
+                    hop(d, js[d], t, n - 1 + step).start()
+
             return 0
 
         return lax.fori_loop(0, down_tiles, tile, 0)
 
-    lax.fori_loop(1, n, gather_step, 0)
+    lax.fori_loop(1, last + 1, gather_step, 0)
+
+
+def write_gathered(n, y, out, sem):
+    me = lax.axis_index(AXIS)
+    last = gathered(n)
+    half = y.shape[0] // (2 * n)
+
+    def each(act):
+        def step(a, _):
+            for d, j in enumerate((lax.rem(me + n - a, n), lax.rem(me + a, n))):
+                block = half_rows(half, d, j)
+                act(pltpu.make_async_copy(y.at[block, :], out.at[block, :], sem.at[d, a]))
+            return 0
+
+        lax.fori_loop(0, last + 1, step, 0)
+
+    each(lambda copy: copy.start())
+    each(lambda copy: copy.wait())
+
+
+def last_hop(n, y, _, held, send_sem, recv_sem):
+    me = lax.axis_index(AXIS)
+    half = held.shape[1]
+    neighbours = (lax.rem(me + 1, n), lax.rem(me + n - 1, n))
+    js = (lax.rem(me + 2, n), lax.rem(me + n - 2, n))
+
+    @pl.when(gathered(n) < n - 1)
+    def _():
+        barrier = greet(me, n)
+        pl.semaphore_wait(barrier, 2)
+        hops = [
+            pltpu.make_async_remote_copy(
+                src_ref=y.at[half_rows(half, d, js[d]), :],
+                dst_ref=held.at[d],
+                send_sem=send_sem.at[d],
+                recv_sem=recv_sem.at[d],
+                device_id={AXIS: neighbours[d]},
+                device_id_type=MESH,
+            )
+            for d in (0, 1)
+        ]
+        for hop in hops:
+            hop.start()
+        for hop in hops:
+            hop.wait()
+
+
+def write_last(n, held, _, out, sem):
+    me = lax.axis_index(AXIS)
+    half = held.shape[1]
+    js = (lax.rem(me + 1, n), lax.rem(me + n - 1, n))
+
+    @pl.when(gathered(n) < n - 1)
+    def _():
+        copies = [
+            pltpu.make_async_copy(held.at[d], out.at[half_rows(half, d, js[d]), :], sem.at[d]) for d in (0, 1)
+        ]
+        for copy in copies:
+            copy.start()
+        for copy in copies:
+            copy.wait()
 
 
 def solution(mesh):
@@ -184,15 +263,45 @@
                 pltpu.SemaphoreType.DMA((2,)),
                 pltpu.SemaphoreType.DMA((2, up_tiles)),
                 pltpu.SemaphoreType.DMA((down_tiles,)),
-                pltpu.SemaphoreType.DMA((2, n, down_tiles)),
-                pltpu.SemaphoreType.DMA((2, n, down_tiles)),
+                pltpu.SemaphoreType.DMA((2, down_tiles)),
+                pltpu.SemaphoreType.DMA((2, 2, down_tiles)),
             ],
             compiler_params=pltpu.CompilerParams(
                 collective_id=0, has_side_effects=True, vmem_limit_bytes=47 << 20
             ),
             name="mlp_ring",
         )(x, w_gate, w_up, w_down)
-        return y
+        in_vmem, anywhere = pl.BlockSpec(memory_space=pltpu.VMEM), pl.BlockSpec(memory_space=pl.ANY)
+        y = pltpu.with_memory_space_constraint(y, pltpu.VMEM)
+        whole = jax.ShapeDtypeStruct((tokens, d_model), jnp.bfloat16)
+        out = pl.pallas_call(
+            functools.partial(write_gathered, n),
+            out_shape=whole,
+            in_specs=[in_vmem],
+            out_specs=anywhere,
+            scratch_shapes=[pltpu.SemaphoreType.DMA((2, n))],
+            compiler_params=pltpu.CompilerParams(vmem_limit_bytes=1 << 20),
+            name="write_gathered",
+        )(y)
+        held = pl.pallas_call(
+            functools.partial(last_hop, n),
+            out_shape=pltpu.VMEM((2, block // 2, d_model), jnp.bfloat16),
+            in_specs=[in_vmem, pl.BlockSpec(memory_space=pltpu.HBM)],
+            out_specs=in_vmem,
+            scratch_shapes=[pltpu.SemaphoreType.DMA((2,)), pltpu.SemaphoreType.DMA((2,))],
+            compiler_params=pltpu.CompilerParams(collective_id=1, has_side_effects=True, vmem_limit_bytes=1 << 20),
+            name="last_hop",
+        )(y, pltpu.with_memory_space_constraint(out, pltpu.HBM))
+        return pl.pallas_call(
+            functools.partial(write_last, n),
+            out_shape=whole,
+            in_specs=[in_vmem, anywhere],
+            out_specs=anywhere,
+            scratch_shapes=[pltpu.SemaphoreType.DMA((2,))],
+            input_output_aliases={1: 0},
+            compiler_params=pltpu.CompilerParams(vmem_limit_bytes=1 << 20),
+            name="write_last",
+        )(pltpu.with_memory_space_constraint(held, pltpu.VMEM), out)
 
     return jax.shard_map(
         step,

time: 345 us -> 338 us (0.980)
  local copies, waits for them, and re-layouts: 6.16 us -> 0 us
    pallas_call x1, Pallas kernels: 338 us -> 314 us  [step(): pl.pallas_call(functools.partial(kernel, n), out_shape=pltpu.VMEM((tokens...]
    pallas_call x0 -> x3, Pallas kernels: none -> 23.7 us  [the longest x1 17 us: step(): pl.pallas_call(functools.partial(last_hop, n), out_shape=pltpu.VMEM((2, b...]
    unnamed x1 -> x0, local copies, waits for them, and re-layouts: 6.16 us -> none
where the time goes in v2:
time: 338 us
  Pallas kernels  338 us (100%)
    pallas_call x1, Pallas kernels, step(): pl.pallas_call(functools.partial(kernel, n), out_shape=pltpu.VMEM((tokens...  314 us
    pallas_call x1, Pallas kernels, step(): pl.pallas_call(functools.partial(last_hop, n), out_shape=pltpu.VMEM((2, b...  17 us

profile of v2, /device:TPU:21, one launch (start us, length us, event | category | flops | bytes accessed | tf_op | source)
XLA Modules:
  0.0 337.8 jit_solution(11996532354048114753)
XLA Ops:
  0.0 314.0 %mlp_ring.1.y = bf16[2048,4096]{1,0:T(8,128)(2,1)S(1)} custom-call(bf16[2048,4096]{1,0:T(8,128)(2,1)} %x_hbm.1, bf16[4096,1792]{1,0:T(8,128)(2,1)} %wg_hbm.1, bf16[4096,1792]{1,0:T(8,128)(2,1)} %wu_hbm.1, bf16[1792,4096]{1,0:T(8,128)(2,1)} %wd_hbm.1), custom_call_target="tpu_custom_call" | custom-call | tf_op jit(solution)/shard_map/mlp_ring/pallas_call | solution.py:252
  314.0 5.3 %write_gathered.1._ = bf16[2048,4096]{1,0:T(8,128)(2,1)} custom-call(bf16[2048,4096]{1,0:T(8,128)(2,1)S(1)} %mlp_ring.1.y), custom_call_target="tpu_custom_call" | custom-call | tf_op jit(solution)/shard_map/write_gathered/pallas_call | solution.py:277
  319.4 17.0 %last_hop.1.held = bf16[2,128,4096]{2,1,0:T(8,128)(2,1)S(1)} custom-call(bf16[2048,4096]{1,0:T(8,128)(2,1)S(1)} %mlp_ring.1.y, bf16[2048,4096]{1,0:T(8,128)(2,1)} %write_gathered.1._), custom_call_target="tpu_custom_call" | custom-call | tf_op jit(solution)/shard_map/last_hop/pallas_call | solution.py:286
  336.4 1.4 write_last.1

commit v3 on v2

--- a/solution.py
+++ b/solution.py
@@ -32,6 +32,7 @@
     me = lax.axis_index(AXIS)
     right, left = lax.rem(me + 1, n), lax.rem(me + n - 1, n)
     half = xv.shape[0] // 2
+    part = half // 2
     up_tiles, _, up_tile = wg.shape
     down_tiles, _, down_tile = wd.shape
 
@@ -40,29 +41,32 @@
             return lax.rem(me + 2 * n - 1 - step, n)
         return lax.rem(me + 1 + step, n)
 
-    def rows(direction, j):
-        return half_rows(half, direction, j)
-
-    def x_copy(direction, step):
-        return pltpu.make_async_copy(
-            x_hbm.at[rows(direction, shard(direction, step)), :],
-            xv.at[pl.ds(direction * half, half), :],
-            x_sem.at[direction],
-        )
+    def part_rows(direction, j, p):
+        return pl.ds(pl.multiple_of(j * 2 * half + direction * half + p * part, part), part)
+
+    def tile_columns(t, size):
+        return pl.ds(pl.multiple_of(t * size, size), size)
+
+    def x_copies(step, p):
+        return [
+            pltpu.make_async_copy(
+                x_hbm.at[part_rows(d, shard(d, step), p), :],
+                xv.at[pl.ds((2 * p + d) * part, part), :],
+                x_sem.at[d, p],
+            )
+            for d in (0, 1)
+        ]
 
     def up_copies(t):
-        columns = pl.ds(pl.multiple_of(t * up_tile, up_tile), up_tile)
         return [
-            pltpu.make_async_copy(hbm.at[:, columns], vmem.at[t], up_sem.at[k, t])
+            pltpu.make_async_copy(hbm.at[:, tile_columns(t, up_tile)], vmem.at[t], up_sem.at[k, t])
             for k, (hbm, vmem) in enumerate(((wg_hbm, wg), (wu_hbm, wu)))
         ]
 
     def down_copy(t):
-        columns = pl.ds(pl.multiple_of(t * down_tile, down_tile), down_tile)
-        return pltpu.make_async_copy(wd_hbm.at[:, columns], wd.at[t], down_sem.at[t])
-
-    def hop(direction, j, t, count):
-        block = y.at[rows(direction, j), pl.ds(pl.multiple_of(t * down_tile, down_tile), down_tile)]
+        return pltpu.make_async_copy(wd_hbm.at[:, tile_columns(t, down_tile)], wd.at[t], down_sem.at[t])
+
+    def send(direction, block, t, count):
         return pltpu.make_async_remote_copy(
             src_ref=block,
             dst_ref=block,
@@ -72,37 +76,75 @@
             device_id_type=MESH,
         )
 
-    def project_up(first):
+    def hop(direction, j, t, count):
+        return send(direction, y.at[half_rows(half, direction, j), tile_columns(t, down_tile)], t, count)
+
+    def first_hop(direction, p, t):
+        rows = part_rows(direction, shard(direction, 0), p)
+        return send(direction, y.at[rows, tile_columns(t, down_tile)], t, 0)
+
+    def project_up(rows, arriving=False, unroll=True):
         def tile(t, _):
-            if first:
+            if arriving:
                 for copy in up_copies(t):
                     copy.wait()
-            gate = jnp.dot(xv[...], wg[t], preferred_element_type=jnp.float32)
-            up = jnp.dot(xv[...], wu[t], preferred_element_type=jnp.float32)
-            columns = pl.ds(pl.multiple_of(t * up_tile, up_tile), up_tile)
-            hidden[:, columns] = (jax.nn.silu(gate) * up).astype(hidden.dtype)
-            return 0
-
-        lax.fori_loop(0, up_tiles, tile, 0)
-
-    def project_down(first, step):
+            gate = jnp.dot(xv[rows, :], wg[t], preferred_element_type=jnp.float32)
+            up = jnp.dot(xv[rows, :], wu[t], preferred_element_type=jnp.float32)
+            hidden[rows, tile_columns(t, up_tile)] = (jax.nn.silu(gate) * up).astype(hidden.dtype)
+            return 0
+
+        lax.fori_loop(0, up_tiles, tile, 0, unroll=unroll and not arriving)
+
+    def project_first_down(p):
+        rows = pl.ds(2 * p * part, 2 * part)
+
+        def start(t):
+            for d in (0, 1):
+                first_hop(d, p, t).start()
+
+        def tiles(ts):
+            if p == 0:
+                for t in ts:
+                    down_copy(t).wait()
+            for t in ts:
+                term = jnp.dot(hidden[rows, :], wd[t], preferred_element_type=jnp.float32)
+                for d in (0, 1):
+                    y[part_rows(d, shard(d, 0), p), tile_columns(t, down_tile)] = term[
+                        d * part : (d + 1) * part, :
+                    ].astype(y.dtype)
+
+        def pair(g, _):
+            tiles((2 * g, 2 * g + 1))
+
+            @pl.when(g > 1)
+            def _():
+                start(2 * g - 2)
+
+            start(2 * g - 1)
+            return 0
+
+        tiles((0,))
+        tiles((1,))
+        start(0)
+        lax.fori_loop(1, down_tiles // 2, pair, 0)
+        start(down_tiles - 2)
+        start(down_tiles - 1)
+
+    def project_down(step):
         js = [shard(d, step) for d in (0, 1)]
         before = [shard(d, step - 1) for d in (0, 1)]
 
         def tile(t, _):
-            if first:
-                down_copy(t).wait()
+            columns = tile_columns(t, down_tile)
             term = jnp.dot(hidden[...], wd[t], preferred_element_type=jnp.float32)
-            columns = pl.ds(pl.multiple_of(t * down_tile, down_tile), down_tile)
-            if not first:
-                for d in (0, 1):
-                    hop(d, js[d], t, step - 1).wait_recv()
-                    hop(d, before[d], t, step - 1).wait_send()
             for d in (0, 1):
-                total = term[d * half : (d + 1) * half, :]
-                if not first:
-                    total = total + y[rows(d, js[d]), columns].astype(jnp.float32)
-                y[rows(d, js[d]), columns] = total.astype(y.dtype)
+                hop(d, js[d], t, step - 1).wait_recv()
+                hop(d, before[d], t, step - 1).wait_send()
+            for d in (0, 1):
+                for p in (0, 1):
+                    rows = part_rows(d, js[d], p)
+                    own = term[(2 * p + d) * part : (2 * p + d + 1) * part, :]
+                    y[rows, columns] = (own + y[rows, columns].astype(jnp.float32)).astype(y.dtype)
 
             @pl.when(t > 0)
             def _():
@@ -117,8 +159,8 @@
 
     barrier = greet(me, n)
 
-    for d in (0, 1):
-        x_copy(d, 0).start()
+    for copy in x_copies(0, 0):
+        copy.start()
 
     def start_up(t, _):
         for copy in up_copies(t):
@@ -132,26 +174,32 @@
         return 0
 
     lax.fori_loop(0, down_tiles, start_down, 0)
-
-    for d in (0, 1):
-        x_copy(d, 0).wait()
-    project_up(True)
-    for d in (0, 1):
-        x_copy(d, 1).start()
-    pl.semaphore_wait(barrier, 2)
-    project_down(True, 0)
+    for copy in x_copies(0, 1):
+        copy.start()
+
+    for p in (0, 1):
+        for copy in x_copies(0, p):
+            copy.wait()
+        project_up(pl.ds(2 * p * part, 2 * part), arriving=p == 0)
+        for copy in x_copies(1, p):
+            copy.start()
+        if p == 0:
+            pl.semaphore_wait(barrier, 2)
+        project_first_down(p)
 
     def reduce_step(step, _):
-        for d in (0, 1):
-            x_copy(d, step).wait()
-        project_up(False)
+        for p in (0, 1):
+            for copy in x_copies(step, p):
+                copy.wait()
+        project_up(pl.ds(0, 2 * half), unroll=False)
 
         @pl.when(step < n - 1)
         def _():
-            for d in (0, 1):
-                x_copy(d, step + 1).start()
-
-        project_down(False, step)
+            for p in (0, 1):
+                for copy in x_copies(step + 1, p):
+                    copy.start()
+
+        project_down(step)
         return 0
 
     lax.fori_loop(1, n, reduce_step, 0)
@@ -247,7 +295,7 @@
         tokens, d_model = x.shape
         hidden = w_gate.shape[1]
         block = tokens // n
-        up_tile, down_tile = 256, 512
+        up_tile, down_tile = 256, 256
         up_tiles, down_tiles = hidden // up_tile, d_model // down_tile
         y = pl.pallas_call(
             functools.partial(kernel, n),
@@ -260,7 +308,7 @@
                 pltpu.VMEM((up_tiles, d_model, up_tile), jnp.bfloat16),
                 pltpu.VMEM((down_tiles, hidden, down_tile), jnp.bfloat16),
                 pltpu.VMEM((block, hidden), jnp.bfloat16),
-                pltpu.SemaphoreType.DMA((2,)),
+                pltpu.SemaphoreType.DMA((2, 2)),
                 pltpu.SemaphoreType.DMA((2, up_tiles)),
                 pltpu.SemaphoreType.DMA((down_tiles,)),
                 pltpu.SemaphoreType.DMA((2, down_tiles)),

time: 338 us -> 336 us (level)
  no operation moved by 1% of the time
where the time goes in v3:
time: 336 us
  Pallas kernels  336 us (100%)
    pallas_call x1, Pallas kernels, step(): pl.pallas_call(functools.partial(kernel, n), out_shape=pltpu.VMEM((tokens...  313 us
    pallas_call x1, Pallas kernels, step(): pl.pallas_call(functools.partial(last_hop, n), out_shape=pltpu.VMEM((2, b...  16.3 us

profile of v3, /device:TPU:21, one launch (start us, length us, event | category | flops | bytes accessed | tf_op | source)
XLA Modules:
  0.0 336.3 jit_solution(13453870321090541978)
XLA Ops:
  0.0 313.3 %mlp_ring.1.y = bf16[2048,4096]{1,0:T(8,128)(2,1)S(1)} custom-call(bf16[2048,4096]{1,0:T(8,128)(2,1)} %x_hbm.1, bf16[4096,1792]{1,0:T(8,128)(2,1)} %wg_hbm.1, bf16[4096,1792]{1,0:T(8,128)(2,1)} %wu_hbm.1, bf16[1792,4096]{1,0:T(8,128)(2,1)} %wd_hbm.1), custom_call_target="tpu_custom_call" | custom-call | tf_op jit(solution)/shard_map/mlp_ring/pallas_call | solution.py:300
  313.3 5.3 %write_gathered.1._ = bf16[2048,4096]{1,0:T(8,128)(2,1)} custom-call(bf16[2048,4096]{1,0:T(8,128)(2,1)S(1)} %mlp_ring.1.y), custom_call_target="tpu_custom_call" | custom-call | tf_op jit(solution)/shard_map/write_gathered/pallas_call | solution.py:325
  318.7 16.3 %last_hop.1.held = bf16[2,128,4096]{2,1,0:T(8,128)(2,1)S(1)} custom-call(bf16[2048,4096]{1,0:T(8,128)(2,1)S(1)} %mlp_ring.1.y, bf16[2048,4096]{1,0:T(8,128)(2,1)} %write_gathered.1._), custom_call_target="tpu_custom_call" | custom-call | tf_op jit(solution)/shard_map/last_hop/pallas_call | solution.py:334
  335.0 1.4 write_last.1

commit v4 on v3

--- a/solution.py
+++ b/solution.py
@@ -8,26 +8,43 @@
 from jax.sharding import PartitionSpec as P
 
 MESH = pl.DeviceIdType.MESH
-AXIS = "tp"
+AXIS, GROUPS = "tp", "dp"
 
 
 def gathered(n):
-    return n - 1 - lax.rem(lax.axis_index("dp"), 2)
+    return n - 1 - lax.rem(lax.axis_index(GROUPS), 2)
 
 
 def half_rows(half, direction, j):
     return pl.ds(pl.multiple_of(j * 2 * half + direction * half, half), half)
 
 
-def greet(me, n):
+def greet(*others):
     barrier = pltpu.get_barrier_semaphore()
-    for neighbour in (lax.rem(me + 1, n), lax.rem(me + n - 1, n)):
-        pl.semaphore_signal(barrier, inc=1, device_id={AXIS: neighbour}, device_id_type=MESH)
+    for other in others:
+        pl.semaphore_signal(barrier, inc=1, device_id=other, device_id_type=MESH)
     return barrier
 
 
 def kernel(
-    n, x_hbm, wg_hbm, wu_hbm, wd_hbm, y, xv, wg, wu, wd, hidden, x_sem, up_sem, down_sem, send_sem, recv_sem
+    n,
+    x_hbm,
+    wg_hbm,
+    wu_hbm,
+    wd_hbm,
+    y,
+    xv,
+    wg,
+    wu,
+    wd,
+    hidden,
+    x_sem,
+    up_sem,
+    down_sem,
+    send_sem,
+    recv_sem,
+    share_send,
+    share_recv,
 ):
     me = lax.axis_index(AXIS)
     right, left = lax.rem(me + 1, n), lax.rem(me + n - 1, n)
@@ -35,6 +52,12 @@
     part = half // 2
     up_tiles, _, up_tile = wg.shape
     down_tiles, _, down_tile = wd.shape
+    group = lax.axis_index(GROUPS)
+    core = lax.rem(group, 2)
+    partner = {GROUPS: group + 1 - 2 * core}
+    split = (up_tiles + 1) // 2
+    first, stop = core * split, split + core * (up_tiles - split)
+    own, other = pl.ds(0, 2 * part), pl.ds(2 * part, 2 * part)
 
     def shard(direction, step):
         if direction == 0:
@@ -83,17 +106,73 @@
         rows = part_rows(direction, shard(direction, 0), p)
         return send(direction, y.at[rows, tile_columns(t, down_tile)], t, 0)
 
-    def project_up(rows, arriving=False, unroll=True):
+    def each_tile(low, high, act):
         def tile(t, _):
-            if arriving:
-                for copy in up_copies(t):
-                    copy.wait()
-            gate = jnp.dot(xv[rows, :], wg[t], preferred_element_type=jnp.float32)
-            up = jnp.dot(xv[rows, :], wu[t], preferred_element_type=jnp.float32)
-            hidden[rows, tile_columns(t, up_tile)] = (jax.nn.silu(gate) * up).astype(hidden.dtype)
-            return 0
-
-        lax.fori_loop(0, up_tiles, tile, 0, unroll=unroll and not arriving)
+            act(t)
+            return 0
+
+        lax.fori_loop(low, high, tile, 0)
+
+    def each_other_tile(act):
+        each_tile(0, first, act)
+        each_tile(stop, up_tiles, act)
+
+    def start_up(t):
+        for copy in up_copies(t):
+            copy.start()
+
+    def wait_up(t):
+        for copy in up_copies(t):
+            copy.wait()
+
+    def share(src, dst, k):
+        return pltpu.make_async_remote_copy(
+            src_ref=src,
+            dst_ref=dst,
+            send_sem=share_send.at[k],
+            recv_sem=share_recv.at[k],
+            device_id=partner,
+            device_id_type=MESH,
+        )
+
+    def share_x():
+        return share(xv.at[own, :], xv.at[other, :], up_tiles)
+
+    def share_hidden(t):
+        columns = tile_columns(t, up_tile)
+        return share(hidden.at[other, columns], hidden.at[own, columns], t)
+
+    def up_tile_of(rows, t):
+        gate = jnp.dot(xv[rows, :], wg[t], preferred_element_type=jnp.float32)
+        up = jnp.dot(xv[rows, :], wu[t], preferred_element_type=jnp.float32)
+        hidden[rows, tile_columns(t, up_tile)] = (jax.nn.silu(gate) * up).astype(hidden.dtype)
+
+    def project_up():
+        each_tile(0, up_tiles, lambda t: up_tile_of(pl.ds(0, 2 * half), t))
+
+    def project_second_up():
+        order = [lax.rem(first + k, up_tiles) for k in range(up_tiles)]
+        present = up_tiles - split
+        for t in order[:present]:
+            up_tile_of(other, t)
+        each_other_tile(wait_up)
+        for t in order[present:]:
+            up_tile_of(other, t)
+
+    def project_shared():
+        wait_up(first)
+        up_tile_of(own, first)
+        share_x().wait_recv()
+        up_tile_of(other, first)
+
+        def tile(t, _):
+            wait_up(t)
+            up_tile_of(pl.ds(0, 2 * half), t)
+            share_hidden(t - 1).start()
+            return 0
+
+        lax.fori_loop(first + 1, stop, tile, 0)
+        share_hidden(stop - 1).start()
 
     def project_first_down(p):
         rows = pl.ds(2 * p * part, 2 * part)
@@ -157,41 +236,40 @@
         for d in (0, 1):
             hop(d, js[d], down_tiles - 1, step).start()
 
-    barrier = greet(me, n)
+    barrier = greet({AXIS: left}, {AXIS: right}, partner)
 
     for copy in x_copies(0, 0):
         copy.start()
-
-    def start_up(t, _):
-        for copy in up_copies(t):
-            copy.start()
-        return 0
-
-    lax.fori_loop(0, up_tiles, start_up, 0)
-
-    def start_down(t, _):
-        down_copy(t).start()
-        return 0
-
-    lax.fori_loop(0, down_tiles, start_down, 0)
+    each_tile(first, stop, start_up)
+    each_tile(0, down_tiles, lambda t: down_copy(t).start())
+
+    for copy in x_copies(0, 0):
+        copy.wait()
+    pl.semaphore_wait(barrier, 3)
+    share_x().start()
+    project_shared()
     for copy in x_copies(0, 1):
         copy.start()
-
-    for p in (0, 1):
-        for copy in x_copies(0, p):
-            copy.wait()
-        project_up(pl.ds(2 * p * part, 2 * part), arriving=p == 0)
-        for copy in x_copies(1, p):
-            copy.start()
-        if p == 0:
-            pl.semaphore_wait(barrier, 2)
-        project_first_down(p)
+    each_other_tile(start_up)
+    each_other_tile(lambda t: share_hidden(t).wait_recv())
+    project_first_down(0)
+
+    for copy in x_copies(0, 1):
+        copy.wait()
+    share_x().wait_send()
+    each_tile(first, stop, lambda t: share_hidden(t).wait_send())
+    for copy in x_copies(1, 0):
+        copy.start()
+    project_second_up()
+    for copy in x_copies(1, 1):
+        copy.start()
+    project_first_down(1)
 
     def reduce_step(step, _):
         for p in (0, 1):
             for copy in x_copies(step, p):
                 copy.wait()
-        project_up(pl.ds(0, 2 * half), unroll=False)
+        project_up()
 
         @pl.when(step < n - 1)
         def _():
@@ -253,7 +331,7 @@
 
     @pl.when(gathered(n) < n - 1)
     def _():
-        barrier = greet(me, n)
+        barrier = greet({AXIS: neighbours[0]}, {AXIS: neighbours[1]})
         pl.semaphore_wait(barrier, 2)
         hops = [
             pltpu.make_async_remote_copy(
@@ -313,9 +391,11 @@
                 pltpu.SemaphoreType.DMA((down_tiles,)),
                 pltpu.SemaphoreType.DMA((2, down_tiles)),
                 pltpu.SemaphoreType.DMA((2, 2, down_tiles)),
+                pltpu.SemaphoreType.DMA((up_tiles + 1,)),
+                pltpu.SemaphoreType.DMA((up_tiles + 1,)),
             ],
             compiler_params=pltpu.CompilerParams(
-                collective_id=0, has_side_effects=True, vmem_limit_bytes=47 << 20
+                collective_id=0, has_side_effects=True, vmem_limit_bytes=50_200_000
             ),
             name="mlp_ring",
         )(x, w_gate, w_up, w_down)

time: 336 us -> 334 us (level)
  no operation moved by 1% of the time
where the time goes in v4:
time: 334 us
  Pallas kernels  334 us (100%)
    pallas_call x1, Pallas kernels, step(): pl.pallas_call(functools.partial(kernel, n), out_shape=pltpu.VMEM((tokens...  312 us
    pallas_call x1, Pallas kernels, step(): pl.pallas_call(functools.partial(last_hop, n), out_shape=pltpu.VMEM((2, b...  15.2 us

profile of v4, /device:TPU:21, one launch (start us, length us, event | category | flops | bytes accessed | tf_op | source)
XLA Modules:
  0.0 334.4 jit_solution(11668391004033378033)
XLA Ops:
  0.0 312.5 %mlp_ring.1.y = bf16[2048,4096]{1,0:T(8,128)(2,1)S(1)} custom-call(bf16[2048,4096]{1,0:T(8,128)(2,1)} %x_hbm.1, bf16[4096,1792]{1,0:T(8,128)(2,1)} %wg_hbm.1, bf16[4096,1792]{1,0:T(8,128)(2,1)} %wu_hbm.1, bf16[1792,4096]{1,0:T(8,128)(2,1)} %wd_hbm.1), custom_call_target="tpu_custom_call" | custom-call | tf_op jit(solution)/shard_map/mlp_ring/pallas_call | solution.py:378
  312.5 5.3 %write_gathered.1._ = bf16[2048,4096]{1,0:T(8,128)(2,1)} custom-call(bf16[2048,4096]{1,0:T(8,128)(2,1)S(1)} %mlp_ring.1.y), custom_call_target="tpu_custom_call" | custom-call | tf_op jit(solution)/shard_map/write_gathered/pallas_call | solution.py:405
  317.9 15.2 %last_hop.1.held = bf16[2,128,4096]{2,1,0:T(8,128)(2,1)S(1)} custom-call(bf16[2048,4096]{1,0:T(8,128)(2,1)S(1)} %mlp_ring.1.y, bf16[2048,4096]{1,0:T(8,128)(2,1)} %write_gathered.1._), custom_call_target="tpu_custom_call" | custom-call | tf_op jit(solution)/shard_map/last_hop/pallas_call | solution.py:414
  333.0 1.4 write_last.1

commit v5 on v4

--- a/solution.py
+++ b/solution.py
@@ -12,7 +12,7 @@
 
 
 def gathered(n):
-    return n - 1 - lax.rem(lax.axis_index(GROUPS), 2)
+    return n - 2 + lax.rem(lax.axis_index(GROUPS), 2)
 
 
 def half_rows(half, direction, j):
@@ -45,6 +45,7 @@
     recv_sem,
     share_send,
     share_recv,
+    told,
 ):
     me = lax.axis_index(AXIS)
     right, left = lax.rem(me + 1, n), lax.rem(me + n - 1, n)
@@ -55,8 +56,9 @@
     group = lax.axis_index(GROUPS)
     core = lax.rem(group, 2)
     partner = {GROUPS: group + 1 - 2 * core}
-    split = (up_tiles + 1) // 2
-    first, stop = core * split, split + core * (up_tiles - split)
+    shared = up_tiles // 2
+    first, theirs = core * (up_tiles - shared), (1 - core) * (up_tiles - shared)
+    between = range(shared, up_tiles - shared)
     own, other = pl.ds(0, 2 * part), pl.ds(2 * part, 2 * part)
 
     def shard(direction, step):
@@ -113,10 +115,6 @@
 
         lax.fori_loop(low, high, tile, 0)
 
-    def each_other_tile(act):
-        each_tile(0, first, act)
-        each_tile(stop, up_tiles, act)
-
     def start_up(t):
         for copy in up_copies(t):
             copy.start()
@@ -151,15 +149,13 @@
         each_tile(0, up_tiles, lambda t: up_tile_of(pl.ds(0, 2 * half), t))
 
     def project_second_up():
-        order = [lax.rem(first + k, up_tiles) for k in range(up_tiles)]
-        present = up_tiles - split
-        for t in order[:present]:
+        for t in [first + k for k in range(shared)] + list(between):
             up_tile_of(other, t)
-        each_other_tile(wait_up)
-        for t in order[present:]:
-            up_tile_of(other, t)
+        each_tile(theirs, theirs + shared, wait_up)
+        each_tile(theirs, theirs + shared, lambda t: up_tile_of(other, t))
 
     def project_shared():
+        last = first + shared - 1
         wait_up(first)
         up_tile_of(own, first)
         share_x().wait_recv()
@@ -171,11 +167,25 @@
             share_hidden(t - 1).start()
             return 0
 
-        lax.fori_loop(first + 1, stop, tile, 0)
-        share_hidden(stop - 1).start()
+        lax.fori_loop(first + 1, last, tile, 0)
+        wait_up(last)
+        up_tile_of(other, last)
+        for t in (last - 1, last):
+            share_hidden(t).start()
+
+        @pl.when(core == 1)
+        def _():
+            pl.semaphore_wait(barrier, 4)
+            pl.semaphore_signal(told, inc=1, device_id=partner, device_id_type=MESH)
+
+        up_tile_of(own, last)
+        for t in between:
+            wait_up(t)
+            up_tile_of(own, t)
 
     def project_first_down(p):
         rows = pl.ds(2 * p * part, 2 * part)
+        singles = 4 if p == 0 else 2
 
         def start(t):
             for d in (0, 1):
@@ -192,10 +202,15 @@
                         d * part : (d + 1) * part, :
                     ].astype(y.dtype)
 
+        def single(t, _):
+            tiles((t,))
+            start(t - 1)
+            return 0
+
         def pair(g, _):
             tiles((2 * g, 2 * g + 1))
 
-            @pl.when(g > 1)
+            @pl.when(2 * g > singles)
             def _():
                 start(2 * g - 2)
 
@@ -203,9 +218,8 @@
             return 0
 
         tiles((0,))
-        tiles((1,))
-        start(0)
-        lax.fori_loop(1, down_tiles // 2, pair, 0)
+        lax.fori_loop(1, singles, single, 0)
+        lax.fori_loop(singles // 2, down_tiles // 2, pair, 0)
         start(down_tiles - 2)
         start(down_tiles - 1)
 
@@ -236,28 +250,48 @@
         for d in (0, 1):
             hop(d, js[d], down_tiles - 1, step).start()
 
-    barrier = greet({AXIS: left}, {AXIS: right}, partner)
+    listener = group - core + 1
+    barrier = greet({AXIS: left, GROUPS: listener}, {AXIS: right, GROUPS: listener})
+
+    @pl.when(core == 1)
+    def _():
+        pl.semaphore_signal(barrier, inc=1, device_id=partner, device_id_type=MESH)
 
     for copy in x_copies(0, 0):
         copy.start()
-    each_tile(first, stop, start_up)
+    each_tile(first, first + shared, start_up)
+    for t in between:
+        start_up(t)
     each_tile(0, down_tiles, lambda t: down_copy(t).start())
+
+    @pl.when(core == 0)
+    def _():
+        pl.semaphore_wait(barrier, 1)
+        pl.semaphore_signal(told, inc=1, device_id=partner, device_id_type=MESH)
+
+    @pl.when(core == 1)
+    def _():
+        pl.semaphore_wait(told, 1)
 
     for copy in x_copies(0, 0):
         copy.wait()
-    pl.semaphore_wait(barrier, 3)
     share_x().start()
     project_shared()
+
+    @pl.when(core == 0)
+    def _():
+        pl.semaphore_wait(told, 1)
+
     for copy in x_copies(0, 1):
         copy.start()
-    each_other_tile(start_up)
-    each_other_tile(lambda t: share_hidden(t).wait_recv())
+    each_tile(theirs, theirs + shared, start_up)
+    each_tile(theirs, theirs + shared, lambda t: share_hidden(t).wait_recv())
     project_first_down(0)
 
     for copy in x_copies(0, 1):
         copy.wait()
     share_x().wait_send()
-    each_tile(first, stop, lambda t: share_hidden(t).wait_send())
+    each_tile(first, first + shared, lambda t: share_hidden(t).wait_send())
     for copy in x_copies(1, 0):
         copy.start()
     project_second_up()
@@ -393,6 +427,7 @@
                 pltpu.SemaphoreType.DMA((2, 2, down_tiles)),
                 pltpu.SemaphoreType.DMA((up_tiles + 1,)),
                 pltpu.SemaphoreType.DMA((up_tiles + 1,)),
+                pltpu.SemaphoreType.REGULAR,
             ],
             compiler_params=pltpu.CompilerParams(
                 collective_id=0, has_side_effects=True, vmem_limit_bytes=50_200_000

time: 334 us -> 334 us (level); the launches traced: 334 us -> 329 us
  Pallas kernels: 334 us -> 329 us
    pallas_call x1, Pallas kernels: 15.2 us -> 0.1 us  [step(): pl.pallas_call(functools.partial(last_hop, n), out_shape=pltpu.VMEM((2, b...]
    pallas_call x1, Pallas kernels: 312 us -> 322 us  [step(): pl.pallas_call(functools.partial(kernel, n), out_shape=pltpu.VMEM((tokens...]
where the time goes in v5:
time: 334 us; the launch traced here: 329 us
  Pallas kernels  329 us (99%)
    pallas_call x1, Pallas kernels, step(): pl.pallas_call(functools.partial(kernel, n), out_shape=pltpu.VMEM((tokens...  322 us

profile of v5, /device:TPU:21, one launch (start us, length us, event | category | flops | bytes accessed | tf_op | source)
XLA Modules:
  0.0 328.6 jit_solution(6093837476652446347)
XLA Ops:
  0.0 322.4 %mlp_ring.1.y = bf16[2048,4096]{1,0:T(8,128)(2,1)S(1)} custom-call(bf16[2048,4096]{1,0:T(8,128)(2,1)} %x_hbm.1, bf16[4096,1792]{1,0:T(8,128)(2,1)} %wg_hbm.1, bf16[4096,1792]{1,0:T(8,128)(2,1)} %wu_hbm.1, bf16[1792,4096]{1,0:T(8,128)(2,1)} %wd_hbm.1), custom_call_target="tpu_custom_call" | custom-call | tf_op jit(solution)/shard_map/mlp_ring/pallas_call | solution.py:412
  322.5 6.0 %write_gathered.1._ = bf16[2048,4096]{1,0:T(8,128)(2,1)} custom-call(bf16[2048,4096]{1,0:T(8,128)(2,1)S(1)} %mlp_ring.1.y), custom_call_target="tpu_custom_call" | custom-call | tf_op jit(solution)/shard_map/write_gathered/pallas_call | solution.py:440
  328.4 0.1 last_hop.1.held
  (1 shorter events, 0.0 us)

commit v6 on v5

--- a/solution.py
+++ b/solution.py
@@ -40,7 +40,6 @@
     hidden,
     x_sem,
     up_sem,
-    down_sem,
     send_sem,
     recv_sem,
     share_send,
@@ -82,14 +81,14 @@
             for d in (0, 1)
         ]
 
-    def up_copies(t):
+    def up_copies(t, slot):
         return [
-            pltpu.make_async_copy(hbm.at[:, tile_columns(t, up_tile)], vmem.at[t], up_sem.at[k, t])
+            pltpu.make_async_copy(hbm.at[:, tile_columns(t, up_tile)], vmem.at[t], up_sem.at[k, slot])
             for k, (hbm, vmem) in enumerate(((wg_hbm, wg), (wu_hbm, wu)))
         ]
 
     def down_copy(t):
-        return pltpu.make_async_copy(wd_hbm.at[:, tile_columns(t, down_tile)], wd.at[t], down_sem.at[t])
+        return pltpu.make_async_copy(wd_hbm.at[:, tile_columns(t, down_tile)], wd.at[t], send_sem.at[0, t])
 
     def send(direction, block, t, count):
         return pltpu.make_async_remote_copy(
@@ -115,12 +114,12 @@
 
         lax.fori_loop(low, high, tile, 0)
 
-    def start_up(t):
-        for copy in up_copies(t):
+    def start_up(t, slot):
+        for copy in up_copies(t, slot):
             copy.start()
 
-    def wait_up(t):
-        for copy in up_copies(t):
+    def wait_up(t, slot):
+        for copy in up_copies(t, slot):
             copy.wait()
 
     def share(src, dst, k):
@@ -134,11 +133,11 @@
         )
 
     def share_x():
-        return share(xv.at[own, :], xv.at[other, :], up_tiles)
-
-    def share_hidden(t):
-        columns = tile_columns(t, up_tile)
-        return share(hidden.at[other, columns], hidden.at[own, columns], t)
+        return share(xv.at[own, :], xv.at[other, :], shared)
+
+    def share_hidden(base, k):
+        columns = tile_columns(base + k, up_tile)
+        return share(hidden.at[other, columns], hidden.at[own, columns], k)
 
     def up_tile_of(rows, t):
         gate = jnp.dot(xv[rows, :], wg[t], preferred_element_type=jnp.float32)
@@ -151,27 +150,27 @@
     def project_second_up():
         for t in [first + k for k in range(shared)] + list(between):
             up_tile_of(other, t)
-        each_tile(theirs, theirs + shared, wait_up)
+        each_tile(0, shared, lambda k: wait_up(theirs + k, k))
         each_tile(theirs, theirs + shared, lambda t: up_tile_of(other, t))
 
     def project_shared():
         last = first + shared - 1
-        wait_up(first)
+        wait_up(first, 0)
         up_tile_of(own, first)
         share_x().wait_recv()
         up_tile_of(other, first)
 
         def tile(t, _):
-            wait_up(t)
+            wait_up(t, t - first)
             up_tile_of(pl.ds(0, 2 * half), t)
-            share_hidden(t - 1).start()
+            share_hidden(first, t - 1 - first).start()
             return 0
 
         lax.fori_loop(first + 1, last, tile, 0)
-        wait_up(last)
+        wait_up(last, shared - 1)
         up_tile_of(other, last)
-        for t in (last - 1, last):
-            share_hidden(t).start()
+        for k in (shared - 2, shared - 1):
+            share_hidden(first, k).start()
 
         @pl.when(core == 1)
         def _():
@@ -180,7 +179,7 @@
 
         up_tile_of(own, last)
         for t in between:
-            wait_up(t)
+            wait_up(t, t)
             up_tile_of(own, t)
 
     def project_first_down(p):
@@ -259,9 +258,9 @@
 
     for copy in x_copies(0, 0):
         copy.start()
-    each_tile(first, first + shared, start_up)
+    each_tile(0, shared, lambda k: start_up(first + k, k))
     for t in between:
-        start_up(t)
+        start_up(t, t)
     each_tile(0, down_tiles, lambda t: down_copy(t).start())
 
     @pl.when(core == 0)
@@ -284,14 +283,14 @@
 
     for copy in x_copies(0, 1):
         copy.start()
-    each_tile(theirs, theirs + shared, start_up)
-    each_tile(theirs, theirs + shared, lambda t: share_hidden(t).wait_recv())
+    each_tile(0, shared, lambda k: start_up(theirs + k, k))
+    each_tile(0, shared, lambda k: share_hidden(theirs, k).wait_recv())
     project_first_down(0)
 
     for copy in x_copies(0, 1):
         copy.wait()
     share_x().wait_send()
-    each_tile(first, first + shared, lambda t: share_hidden(t).wait_send())
+    each_tile(0, shared, lambda k: share_hidden(first, k).wait_send())
     for copy in x_copies(1, 0):
         copy.start()
     project_second_up()
@@ -421,12 +420,11 @@
                 pltpu.VMEM((down_tiles, hidden, down_tile), jnp.bfloat16),
                 pltpu.VMEM((block, hidden), jnp.bfloat16),
                 pltpu.SemaphoreType.DMA((2, 2)),
-                pltpu.SemaphoreType.DMA((2, up_tiles)),
-                pltpu.SemaphoreType.DMA((down_tiles,)),
+                pltpu.SemaphoreType.DMA((2, up_tiles - up_tiles // 2)),
                 pltpu.SemaphoreType.DMA((2, down_tiles)),
                 pltpu.SemaphoreType.DMA((2, 2, down_tiles)),
-                pltpu.SemaphoreType.DMA((up_tiles + 1,)),
-                pltpu.SemaphoreType.DMA((up_tiles + 1,)),
+                pltpu.SemaphoreType.DMA((up_tiles // 2 + 1,)),
+                pltpu.SemaphoreType.DMA((up_tiles // 2 + 1,)),
                 pltpu.SemaphoreType.REGULAR,
             ],
             compiler_params=pltpu.CompilerParams(

time: 334 us -> 333 us (level)
  no operation moved by 1% of the time
where the time goes in v6:
time: 333 us; the launch traced here: 328 us
  Pallas kernels  328 us (98%)
    pallas_call x1, Pallas kernels, step(): pl.pallas_call(functools.partial(kernel, n), out_shape=pltpu.VMEM((tokens...  322 us

profile of v6, /device:TPU:21, one launch (start us, length us, event | category | flops | bytes accessed | tf_op | source)
XLA Modules:
  0.0 328.3 jit_solution(14292008858561013841)
XLA Ops:
  0.0 322.2 %mlp_ring.1.y = bf16[2048,4096]{1,0:T(8,128)(2,1)S(1)} custom-call(bf16[2048,4096]{1,0:T(8,128)(2,1)} %x_hbm.1, bf16[4096,1792]{1,0:T(8,128)(2,1)} %wg_hbm.1, bf16[4096,1792]{1,0:T(8,128)(2,1)} %wu_hbm.1, bf16[1792,4096]{1,0:T(8,128)(2,1)} %wd_hbm.1), custom_call_target="tpu_custom_call" | custom-call | tf_op jit(solution)/shard_map/mlp_ring/pallas_call | solution.py:411
  322.2 6.0 %write_gathered.1._ = bf16[2048,4096]{1,0:T(8,128)(2,1)} custom-call(bf16[2048,4096]{1,0:T(8,128)(2,1)S(1)} %mlp_ring.1.y), custom_call_target="tpu_custom_call" | custom-call | tf_op jit(solution)/shard_map/write_gathered/pallas_call | solution.py:438
  328.2 0.1 last_hop.1.held
  (1 shorter events, 0.0 us)

commit v7 on v6

--- a/solution.py
+++ b/solution.py
@@ -249,18 +249,19 @@
         for d in (0, 1):
             hop(d, js[d], down_tiles - 1, step).start()
 
-    listener = group - core + 1
-    barrier = greet({AXIS: left, GROUPS: listener}, {AXIS: right, GROUPS: listener})
-
-    @pl.when(core == 1)
-    def _():
-        pl.semaphore_signal(barrier, inc=1, device_id=partner, device_id_type=MESH)
-
     for copy in x_copies(0, 0):
         copy.start()
     each_tile(0, shared, lambda k: start_up(first + k, k))
     for t in between:
         start_up(t, t)
+
+    listener = group - core + 1
+    barrier = greet({AXIS: left, GROUPS: listener}, {AXIS: right, GROUPS: listener})
+
+    @pl.when(core == 1)
+    def _():
+        pl.semaphore_signal(barrier, inc=1, device_id=partner, device_id_type=MESH)
+
     each_tile(0, down_tiles, lambda t: down_copy(t).start())
 
     @pl.when(core == 0)

time: 333 us -> 333 us (level)
  no operation moved by 1% of the time
where the time goes in v7:
time: 333 us; the launch traced here: 328 us
  Pallas kernels  328 us (98%)
    pallas_call x1, Pallas kernels, step(): pl.pallas_call(functools.partial(kernel, n), out_shape=pltpu.VMEM((tokens...  322 us

profile of v7, /device:TPU:21, one launch (start us, length us, event | category | flops | bytes accessed | tf_op | source)
XLA Modules:
  0.0 328.3 jit_solution(14647312021486308879)
XLA Ops:
  0.0 322.2 %mlp_ring.1.y = bf16[2048,4096]{1,0:T(8,128)(2,1)S(1)} custom-call(bf16[2048,4096]{1,0:T(8,128)(2,1)} %x_hbm.1, bf16[4096,1792]{1,0:T(8,128)(2,1)} %wg_hbm.1, bf16[4096,1792]{1,0:T(8,128)(2,1)} %wu_hbm.1, bf16[1792,4096]{1,0:T(8,128)(2,1)} %wd_hbm.1), custom_call_target="tpu_custom_call" | custom-call | tf_op jit(solution)/shard_map/mlp_ring/pallas_call | solution.py:412
  322.2 6.0 %write_gathered.1._ = bf16[2048,4096]{1,0:T(8,128)(2,1)} custom-call(bf16[2048,4096]{1,0:T(8,128)(2,1)S(1)} %mlp_ring.1.y), custom_call_target="tpu_custom_call" | custom-call | tf_op jit(solution)/shard_map/write_gathered/pallas_call | solution.py:439
  328.2 0.1 last_hop.1.held
  (1 shorter events, 0.0 us)
